TPU v7x, 32 devices: a whole 2x2x4 slice. The times are simulated.
32 devices in a mesh: dp: 8 (over z, x), patch: 4 (over y, core).
Axes of the slice: x: 2, y: 2, z: 4, core: 2. Of those that a mesh axis runs over, the one named last changes fastest.
Arguments:
- token_ids: int32 [128], replicated, may hold values from 0 to 31999
- parents: int32 [128], replicated, may hold values from 0 to 3
- embedding: bfloat16 [32000, 1024], P('dp'), may hold values from -6 to 6
- self_gain: bfloat16 [1024], replicated, may hold values from 0.25 to 1.75
- query_weight: bfloat16 [1024, 1024], P(None, 'patch'), may hold values from -0.1875 to 0.1875
- key_weight: bfloat16 [1024, 1024], P(None, 'patch'), may hold values from -0.1875 to 0.1875
- value_weight: bfloat16 [1024, 1024], P(None, 'patch'), may hold values from -0.1875 to 0.1875
- output_weight: bfloat16 [1024, 1024], P('patch'), may hold values from -0.75 to 0.75
- past_keys: bfloat16 [128, 128, 1024], P('dp', None, 'patch'), may hold values from -200 to 200
- past_values: bfloat16 [128, 128, 1024], P('dp', None, 'patch'), may hold values from -6 to 6
- cross_gain: bfloat16 [1024], replicated, may hold values from 0.25 to 1.75
- cross_query: bfloat16 [1024, 1024], replicated, may hold values from -0.1875 to 0.1875
- cross_output: bfloat16 [1024, 1024], replicated, may hold values from -0.75 to 0.75
- image_keys: bfloat16 [8, 16, 256, 1024], P('dp', None, 'patch'), may hold values from -260 to 260
- image_values: bfloat16 [8, 16, 256, 1024], P('dp', None, 'patch'), may hold values from -6 to 6
Outputs:
- hidden: bfloat16 [128, 1024], P('dp')
- new_keys: bfloat16 [128, 1024], P('dp', 'patch')
- new_values: bfloat16 [128, 1024], P('dp', 'patch')
Inputs may be any that keep to these rules, and one draw needn't show every extreme that they name: `parents`: a beam of the row's own image.
All inputs are finite; a program needn't handle non-finite values.
Results may differ from a plain program's by a relative error of at most 0.019.
The roundings to bfloat16 on the way count: a program that leaves them out, or rounds other values in their place, can miss the bound.
Values may be sent and summed in bfloat16 or wider, within the bound.
No kernel may reach another device: no remote copies, remote signals or barrier semaphores. Data moves between devices by JAX's collectives and lax.ppermute only.
A program may use at most 64 MiB of HBM per device.

v0:
```python
import math
import jax
import jax.numpy as jnp
from jax import lax
from jax.sharding import PartitionSpec as P

D = 1024
HEADS = 16
BEAMS = 4


def from_partner(value, axis, distance):
    mask = 2**distance
    pairs = [(source, source ^ mask) for source in range(lax.axis_size(axis))]
    return lax.ppermute(value, axis, pairs)


def joined(x, axis, combine):
    everything = jax.tree.map(lambda part: lax.all_gather(part, axis), x)
    first = jax.tree.map(lambda part: part[0], everything)

    def step(k, so_far):
        return combine(so_far, jax.tree.map(lambda part: part[k], everything))

    return lax.fori_loop(1, lax.axis_size(axis), step, first)


def normalize(inputs, gains):
    factor = lax.rsqrt(jnp.mean(inputs * inputs, axis=-1, keepdims=True) + 1e-06)
    return (inputs * factor * gains.astype(jnp.float32)).astype(jnp.bfloat16)


def combine(former, latter):
    peak_former, total_former, sum_former = former
    peak_latter, total_latter, sum_latter = latter
    peaks = jnp.maximum(peak_former, peak_latter)
    former_scale = jnp.exp(peak_former - peaks)
    latter_scale = jnp.exp(peak_latter - peaks)
    heads_count = peaks.shape[-1]
    count_rows = peaks.shape[0]
    sums = (
        sum_former.reshape(count_rows, heads_count, -1) * former_scale[..., None]
        + sum_latter.reshape(count_rows, heads_count, -1) * latter_scale[..., None]
    )
    return (
        peaks,
        total_former * former_scale + total_latter * latter_scale,
        sums.reshape(count_rows, -1),
    )


def beam_collect(pieces, concat_dim):
    for bit_index in range(2):
        partner = from_partner(pieces, "dp", bit_index)
        upper_bit = lax.axis_index("dp") // 2**bit_index % 2
        pieces = jnp.where(
            upper_bit == 1,
            jnp.concatenate([partner, pieces], concat_dim),
            jnp.concatenate([pieces, partner], concat_dim),
        )
    return pieces


def beam_reduce(partial_value):
    for bit_index in (1, 0):
        upper_bit = lax.axis_index("dp") // 2**bit_index % 2
        half_rows = partial_value[0].shape[0] // 2
        keep_part = tuple(
            (
                lax.dynamic_slice_in_dim(member, upper_bit * half_rows, half_rows, 0)
                for member in partial_value
            )
        )
        send_part = tuple(
            (
                lax.dynamic_slice_in_dim(member, (1 - upper_bit) * half_rows, half_rows, 0)
                for member in partial_value
            )
        )
        received = from_partner(send_part, "dp", bit_index)
        partial_value = combine(keep_part, received)
    return partial_value


def patch_merge(partial_value):
    return joined(partial_value, "patch", combine)


def shards(
    token_ids,
    parents,
    embedding,
    self_gain,
    query_weight,
    key_weight,
    value_weight,
    output_weight,
    past_keys,
    past_values,
    cross_gain,
    cross_query,
    cross_output,
    image_keys,
    image_values,
):
    row_count = past_keys.shape[0]
    length = past_keys.shape[1]
    width_here = query_weight.shape[1]
    head_size = D // HEADS
    heads_here = width_here // head_size
    scaling = 1.0 / math.sqrt(head_size)
    position = lax.axis_index("dp")
    slab = embedding.shape[0]
    vocab_ids = position * slab + jnp.arange(slab, dtype=jnp.int32)
    onehot_table = (token_ids[:, None] == vocab_ids[None, :]).astype(jnp.bfloat16)
    tokens = lax.psum_scatter(
        jnp.dot(onehot_table, embedding, preferred_element_type=jnp.float32),
        "dp",
        scatter_dimension=0,
        tiled=True,
    )
    normed = normalize(tokens, self_gain)
    queries = jnp.dot(normed, query_weight, preferred_element_type=jnp.float32).astype(jnp.bfloat16)
    new_key = jnp.dot(normed, key_weight, preferred_element_type=jnp.float32).astype(jnp.bfloat16)
    new_value = jnp.dot(normed, value_weight, preferred_element_type=jnp.float32).astype(
        jnp.bfloat16
    )
    query_heads = queries.reshape(row_count, heads_here, head_size)
    key_heads = new_key.reshape(row_count, heads_here, head_size)
    value_heads = new_value.reshape(row_count, heads_here, head_size)
    own_score = (
        jnp.sum(query_heads.astype(jnp.float32) * key_heads.astype(jnp.float32), axis=-1) * scaling
    )
    paired = jnp.stack([queries, new_key], 0)
    gathered = beam_collect(paired, 1).reshape(2, BEAMS, row_count, heads_here, head_size)
    gathered_queries = gathered[0]
    gathered_keys = gathered[1]
    own_every = (
        jnp.sum(gathered_queries.astype(jnp.float32) * gathered_keys.astype(jnp.float32), axis=-1)
        * scaling
    )
    block_start = position // BEAMS * BEAMS * row_count
    block_parents = lax.dynamic_slice_in_dim(parents, block_start, BEAMS * row_count, 0).reshape(
        BEAMS, row_count
    )
    living = (block_parents == position % BEAMS).astype(jnp.float32)
    old_keys = past_keys.reshape(row_count, length, heads_here, head_size)
    old_values = past_values.reshape(row_count, length, heads_here, head_size)
    scores = (
        jnp.einsum(
            "bihe,ilhe->bihl", gathered_queries, old_keys, preferred_element_type=jnp.float32
        )
        * scaling
    )
    maxima = jnp.maximum(jnp.max(scores, axis=-1), own_every)
    powers = jnp.exp(scores - maxima[..., None]) * living[:, :, None, None]
    totals = jnp.sum(powers, axis=-1) + jnp.exp(own_every - maxima) * living[:, :, None]
    numerators = jnp.einsum(
        "bihl,ilhe->bihe",
        powers.astype(jnp.bfloat16),
        old_values,
        preferred_element_type=jnp.float32,
    )
    partial_value = (
        jnp.where(living[:, :, None] > 0.5, maxima, -1e30).reshape(BEAMS * row_count, heads_here),
        totals.reshape(BEAMS * row_count, heads_here),
        numerators.reshape(BEAMS * row_count, width_here),
    )
    peaks, sums, weighted = beam_reduce(partial_value)
    own_weight = jnp.exp(own_score - peaks).astype(jnp.bfloat16).astype(jnp.float32)
    weighted = weighted.reshape(row_count, heads_here, head_size) + own_weight[
        ..., None
    ] * value_heads.astype(jnp.float32)
    self_context = weighted / sums[..., None]
    self_context = self_context.reshape(row_count, width_here).astype(jnp.bfloat16)
    middle = tokens + lax.psum(
        jnp.dot(self_context, output_weight, preferred_element_type=jnp.float32), "patch"
    )
    probes = jnp.dot(
        normalize(middle, cross_gain), cross_query, preferred_element_type=jnp.float32
    ).astype(jnp.bfloat16)
    every_probe = beam_collect(probes, 0).reshape(BEAMS, row_count, HEADS, head_size)
    patch_count = image_keys.shape[2]
    patch_keys = image_keys.reshape(row_count, patch_count, HEADS, head_size)
    patch_values = image_values.reshape(row_count, patch_count, HEADS, head_size)
    cross_scores = (
        jnp.einsum("bihe,iphe->bihp", every_probe, patch_keys, preferred_element_type=jnp.float32)
        * scaling
    )
    cross_peaks = jnp.max(cross_scores, axis=-1)
    cross_powers = jnp.exp(cross_scores - cross_peaks[..., None])
    cross_totals = jnp.sum(cross_powers, axis=-1)
    cross_sums = jnp.einsum(
        "bihp,iphe->bihe",
        cross_powers.astype(jnp.bfloat16),
        patch_values,
        preferred_element_type=jnp.float32,
    )
    partial_value = (
        cross_peaks.reshape(BEAMS * row_count, HEADS),
        cross_totals.reshape(BEAMS * row_count, HEADS),
        cross_sums.reshape(BEAMS * row_count, D),
    )
    partial_value = beam_reduce(patch_merge(partial_value))
    cross_context = (
        (partial_value[2].reshape(row_count, HEADS, head_size) / partial_value[1][..., None])
        .reshape(row_count, D)
        .astype(jnp.bfloat16)
    )
    hidden = (
        middle + jnp.dot(cross_context, cross_output, preferred_element_type=jnp.float32)
    ).astype(jnp.bfloat16)
    return (hidden, new_key, new_value)


def solution(mesh):
    in_specs = (
        P(),
        P(),
        P("dp", None),
        P(),
        P(None, "patch"),
        P(None, "patch"),
        P(None, "patch"),
        P("patch", None),
        P("dp", None, "patch"),
        P("dp", None, "patch"),
        P(),
        P(),
        P(),
        P("dp", None, "patch", None),
        P("dp", None, "patch", None),
    )
    out_specs = (P("dp", None), P("dp", "patch"), P("dp", "patch"))
    return jax.shard_map(shards, mesh=mesh, in_specs=in_specs, out_specs=out_specs, check_vma=False)
```

profile of v0, /device:TPU:0, one launch (start us, length us, event | category | flops | bytes accessed | tf_op | source)
XLA Modules:
  0.0 208.8 jit_solution(12373102557429961516)
XLA Ops:
  7.3 5.6 %fusion.7 = f32[128,1024]{1,0:T(8,128)} fusion(bf16[4000,1024]{1,0:T(8,128)(2,1)} %param.19, s32[4000]{0:T(1024)S(1)} %iota_add_fusion, s32[128]{0:T(128)} %param.17), kind=kOutput, calls=%fused_computation.12 | convolution fusion | flops 1049088000 | bytes 8732800 | tf_op jit(solution)/shard_map/dot_general | solution.py:117
  13.0 65.4 %reduce-scatter.2.cloned.1.call-done = f32[16,1024]{1,0:T(8,128)} async-done(((f32[128,1024]{1,0:T(8,128)}), f32[16,1024]{1,0:T(8,128)}) %reduce-scatter.2.cloned.1.call-update) | async-done | bytes 65552 | tf_op jit(solution)/shard_map/reduce_scatter | solution.py:116
  78.4 1.0 multiply_reduce_fusion.2
  79.4 0.9 multiply_convert_fusion.1
  80.7 1.4 collective-permute-start
  82.1 1.6 copy.108
  83.9 2.3 %copy.114 = bf16[16,128,256]{1,2,0:T(8,128)(2,1)} copy(bf16[16,128,256]{2,1,0:T(8,128)(2,1)} %param.26) | data formatting | bytes 2097152 | tf_op args[9]
  86.2 1.6 collective-permute-start.1
  87.8 1.2 convolution_convert_fusion.1
  89.2 0.9 collective-permute-done.1
  91.9 1.9 convolution_bitcast_fusion
  94.5 1.6 collective-permute-start.2
  96.5 1.5 collective-permute-start.3
  98.3 1.6 collective-permute-done.6
  100.2 0.6 collective-permute-start.4
  100.8 1.5 collective-permute-start.7
  102.4 0.6 collective-permute-start.5
  102.9 1.0 collective-permute-done.4
  105.2 1.0 collective-permute-done.5
  106.2 0.8 fusion.41
  107.3 29.6 %all-reduce.2.cloned.1.call-done = f32[16,1024]{1,0:T(8,128)} async-done(((f32[16,1024]{1,0:T(8,128)}), f32[16,1024]{1,0:T(8,128)}) %all-reduce.2.cloned.1.call-update) | async-done | bytes 65552 | tf_op jit(solution)/shard_map/psum | solution.py:176
  136.9 1.0 multiply_reduce_fusion.1
  138.3 1.5 collective-permute-start.8
  139.8 2.4 %collective-permute-done.8 = bf16[16,1024]{1,0:T(8,128)(2,1)S(1)} collective-permute-done((bf16[16,1024]{1,0:T(8,128)(2,1)S(1)}, bf16[16,1024]{1,0:T(8,128)(2,1)S(1)}, u32[]{:S(2)}, u32[]{:S(2)}) %collective-permute-start.8) | collective-permute-done | bytes 32800 | tf_op jit(solution)/shard_map/ppermute | solution.py:15
  142.2 1.6 collective-permute-start.9
  143.8 6.4 %reshape.165 = bf16[16,64,16,64]{3,2,1,0:T(8,128)(2,1)} reshape(bf16[1,16,64,1024]{3,2,1,0:T(8,128)(2,1)} %param.30) | data formatting | bytes 4194304 | tf_op jit(solution)/shard_map/reshape | solution.py:184
  150.1 6.4 %reshape.166 = bf16[16,64,16,64]{3,2,1,0:T(8,128)(2,1)} reshape(bf16[1,16,64,1024]{3,2,1,0:T(8,128)(2,1)} %param.31) | data formatting | bytes 4194304 | tf_op jit(solution)/shard_map/reshape | solution.py:185
  156.8 4.7 %fusion.51 = (f32[4,16,16]{0,2,1:T(8,128)S(1)}, f32[4,16,16,64]{3,0,2,1:T(4,128)S(1)}) fusion(bf16[16,64,16,64]{3,2,1,0:T(8,128)(2,1)} %reshape.165, bf16[4,16,16,64]{3,2,1,0:T(8,128)(2,1)S(1)} %select_n.148), kind=kOutput, calls=%fused_computation.109 | convolution fusion | flops 8518656 | bytes 2494464 | tf_op jit(solution)/shard_map/bihe,iphe->bihp/dot_general | solution.py:187
  161.5 1.3 fusion.9
  162.8 0.9 all_gather_reshape.11
  163.9 0.7 fusion.23
  164.9 5.2 %all_gather.10 = f32[4,64,16]{1,2,0:T(8,128)S(1)} all-gather(f32[1,64,16]{1,2,0:T(8,128)S(1)} %all_gather_reshape.10), channel_id=1, replica_groups=mesh['dp'=8,'patch'=4] {'patch'}, dimensions={0}, use_global_device_ids=true | all-gather | bytes 20480 | tf_op jit(solution)/shard_map/all_gather | solution.py:19
  170.1 5.4 %all_gather.9 = f32[4,64,16]{1,2,0:T(8,128)S(1)} all-gather(f32[1,64,16]{1,2,0:T(8,128)S(1)} %all_gather_reshape.9), channel_id=1, replica_groups=mesh['dp'=8,'patch'=4] {'patch'}, dimensions={0}, use_global_device_ids=true | all-gather | bytes 20480 | tf_op jit(solution)/shard_map/all_gather | solution.py:19
  175.5 4.3 %all-gather.2.cloned.1.call-done = f32[4,64,1024]{2,1,0:T(8,128)} async-done(((f32[1,64,1024]{2,1,0:T(8,128)}), f32[4,64,1024]{2,1,0:T(8,128)}) %all-gather.2.cloned.1.call-update) | async-done | bytes 1048592 | tf_op jit(solution)/shard_map/all_gather | solution.py:19
  179.8 1.0 slice_bitcast_fusion
  180.8 6.1 %while.19 = (s32[]{:T(128)}, f32[64,16]{0,1:T(8,128)S(1)}, f32[64,16]{0,1:T(8,128)S(1)}, f32[64,1024]{1,0:T(8,128)S(1)}, f32[4,64,16]{1,2,0:T(8,128)S(1)}, /*ind...) while((s32[]{:T(128)}, f32[64,16]{0,1:T(8,128)S(1)}, ...), condition=%wide.region_11.12_spmd, body=%wide.region_10.11_spmd.sunk | while | flops 202757 | bytes 2941079 | solution.py:25
  181.8 1.1 fusion.67
  183.8 1.1 fusion.67
  185.8 1.1 fusion.67
  187.0 1.5 collective-permute-start.10
  188.6 0.5 collective-permute-start.14
  189.1 1.6 collective-permute-start.11
  190.7 1.6 collective-permute-done.14
  193.1 1.5 collective-permute-start.12
  194.7 0.6 collective-permute-start.15
  195.4 1.5 collective-permute-start.13
  196.9 1.5 collective-permute-done.15
  199.7 2.6 %fusion.19 = bf16[16,1024]{1,0:T(8,128)(2,1)} fusion(f32[16,1024]{1,0:T(8,128)S(1)} %get-tuple-element.210, bf16[1024,1024]{1,0:T(8,128)(2,1)} %param.29, f32[16,1024]{1,0:T(8,128)S(1)} %div.62, f32[16,1024]{1,0:T(8,128)S(1)} %collective-permute-done.13, f32[16,1024]{1,0:T(8,128)S(1)} %mul.400, f32[16,1024]{1,0:T(8,128)S(1)} %mul.397, ...), kind=kOutput, calls=%fused_computation.21 | convolution fusion | flops 33669120 | bytes 2523140 | tf_op jit(solution)/shard_map/dot_general | solution.py:211
  (146 shorter events, 12.2 us)
Async XLA Ops:
  7.2 130.7 %copy-start = (bf16[1024,1024]{1,0:T(8,128)(2,1)S(1)}, bf16[1024,1024]{1,0:T(8,128)(2,1)}, u32[]{:S(2)}) copy-start(bf16[1024,1024]{1,0:T(8,128)(2,1)} %param.28) | copy-start | bytes 6291460
  7.2 71.2 %reduce-scatter.2.cloned.1.call-start = ((), (), s32[]{:S(2)}) async-start(), calls=%async_computation.1 | async-start | bytes 589824 | tf_op jit(solution)/shard_map/reduce_scatter | solution.py:116
  7.2 5.7 %copy-start.8 = (bf16[1024]{0:T(1024)(128)(2,1)S(1)}, bf16[1024]{0:T(1024)(128)(2,1)}, u32[]{:S(2)}) copy-start(bf16[1024]{0:T(1024)(128)(2,1)} %param.20) | copy-start | bytes 6148
  7.3 73.0 %copy-start.5 = (bf16[1024,256]{1,0:T(8,128)(2,1)S(1)}, bf16[1024,256]{1,0:T(8,128)(2,1)}, u32[]{:S(2)}) copy-start(bf16[1024,256]{1,0:T(8,128)(2,1)} %param.21) | copy-start | bytes 1572868
  7.3 73.2 %copy-start.3 = (bf16[1024,256]{1,0:T(8,128)(2,1)S(1)}, bf16[1024,256]{1,0:T(8,128)(2,1)}, u32[]{:S(2)}) copy-start(bf16[1024,256]{1,0:T(8,128)(2,1)} %param.22) | copy-start | bytes 1572868
  7.3 74.8 %copy-start.10 = (s32[128]{0:T(128)S(1)}, s32[128]{0:T(128)}, u32[]{:S(2)}) copy-start(s32[128]{0:T(128)} %param.18) | copy-start | bytes 1540
  12.9 124.0 %all-reduce.2.cloned.1.call-start = ((), (), s32[]{:S(2)}) async-start(), calls=%async_computation.2 | async-start | bytes 131072 | tf_op jit(solution)/shard_map/psum | solution.py:176
  80.7 8.6 %copy-start.6 = (bf16[16,256]{1,0:T(8,128)(2,1)}, bf16[16,256]{1,0:T(8,128)(2,1)S(1)}, u32[]{:S(2)}) copy-start(bf16[16,256]{1,0:T(8,128)(2,1)S(1)} %get-tuple-element.230) | copy-start | bytes 24580
  80.7 5.5 %collective-permute-start = (bf16[2,16,256]{2,1,0:T(8,128)(2,1)S(1)}, bf16[2,16,256]{2,1,0:T(8,128)(2,1)S(1)}, u32[]{:S(2)}, u32[]{:S(2)}) collective-permute-start(bf16[2,16,256]{2,1,0:T(8,128)(2,1)S(1)} %pad_maximum_fusion), channel_id=1, source_target_pairs={{0,4},{4,0},{8,12},{12,8},{16,20},{20,16},{24,28},{28,24},{1,5},{5... | collective-permute-start | bytes 49160 | tf_op jit(solution)/shard_map/ppermute | solution.py:15
  86.2 21.1 %copy-start.9 = (bf16[1024]{0:T(1024)(128)(2,1)S(1)}, bf16[1024]{0:T(1024)(128)(2,1)}, u32[]{:S(2)}) copy-start(bf16[1024]{0:T(1024)(128)(2,1)} %param.27) | copy-start | bytes 6148
  86.2 50.7 %copy-start.2 = (f32[16,1024]{1,0:T(8,128)S(1)}, f32[16,1024]{1,0:T(8,128)}, u32[]{:S(2)}) copy-start(f32[16,1024]{1,0:T(8,128)} %reduce-scatter.2.cloned.1.call-done) | copy-start | bytes 196612
  86.2 4.0 %collective-permute-start.1 = (bf16[2,32,256]{2,1,0:T(8,128)(2,1)S(1)}, bf16[2,32,256]{2,1,0:T(8,128)(2,1)S(1)}, u32[]{:S(2)}, u32[]{:S(2)}) collective-permute-start(bf16[2,32,256]{2,1,0:T(8,128)(2,1)S(1)} %maximum_select_fusion.3), channel_id=1, source_target_pairs={{0,8},{4,12},{8,0},{12,4},{16,24},{20,28},{24,16},{28,20},{1,9},{5... | collective-permute-start | bytes 98312 | tf_op jit(solution)/shard_map/ppermute | solution.py:15
  89.0 49.3 %copy-start.7 = (bf16[16,256]{1,0:T(8,128)(2,1)}, bf16[16,256]{1,0:T(8,128)(2,1)S(1)}, u32[]{:S(2)}) copy-start(bf16[16,256]{1,0:T(8,128)(2,1)S(1)} %convolution_convert_fusion.1) | copy-start | bytes 24580
  90.8 15.4 %copy-start.4 = (bf16[256,1024]{1,0:T(8,128)(2,1)S(1)}, bf16[256,1024]{1,0:T(8,128)(2,1)}, u32[]{:S(2)}) copy-start(bf16[256,1024]{1,0:T(8,128)(2,1)} %param.24) | copy-start | bytes 1572868
  94.5 3.8 %collective-permute-start.2 = (f32[32,4]{1,0:T(8,128)S(1)}, f32[32,4]{1,0:T(8,128)S(1)}, u32[]{:S(2)}, u32[]{:S(2)}) collective-permute-start(f32[32,4]{1,0:T(8,128)S(1)} %constant_dynamic-slice_fusion.11), channel_id=1, source_target_pairs={{0,8},{4,12},{8,0},{12,4},{16,24},{20,28},{24,16},{28,20},{1,9},{5... | collective-permute-start | bytes 1544 | tf_op jit(solution)/shard_map/ppermute | solution.py:15
  96.1 3.7 %collective-permute-start.6 = (f32[32,4]{1,0:T(8,128)S(1)}, f32[32,4]{1,0:T(8,128)S(1)}, u32[]{:S(2)}, u32[]{:S(2)}) collective-permute-start(f32[32,4]{1,0:T(8,128)S(1)} %constant_dynamic-slice_fusion.7), channel_id=1, source_target_pairs={{0,8},{4,12},{8,0},{12,4},{16,24},{20,28},{24,16},{28,20},{1,9},{5... | collective-permute-start | bytes 1544 | tf_op jit(solution)/shard_map/ppermute | solution.py:15
  96.5 5.8 %collective-permute-start.3 = (f32[32,256]{1,0:T(8,128)S(1)}, f32[32,256]{1,0:T(8,128)S(1)}, u32[]{:S(2)}, u32[]{:S(2)}) collective-permute-start(f32[32,256]{1,0:T(8,128)S(1)} %constant_dynamic-slice_fusion.10), channel_id=1, source_target_pairs={{0,8},{4,12},{8,0},{12,4},{16,24},{20,28},{24,16},{28,20},{1,9},{5... | collective-permute-start | bytes 98312 | tf_op jit(solution)/shard_map/ppermute | solution.py:15
  100.2 3.7 %collective-permute-start.4 = (f32[16,4]{1,0:T(8,128)S(1)}, f32[16,4]{1,0:T(8,128)S(1)}, u32[]{:S(2)}, u32[]{:S(2)}) collective-permute-start(f32[16,4]{1,0:T(8,128)S(1)} %constant_dynamic-slice_fusion.9), channel_id=1, source_target_pairs={{0,4},{4,0},{8,12},{12,8},{16,20},{20,16},{24,28},{28,24},{1,5},{5... | collective-permute-start | bytes 776 | tf_op jit(solution)/shard_map/ppermute | solution.py:15
  100.8 3.7 %collective-permute-start.7 = (f32[16,4]{1,0:T(8,128)S(1)}, f32[16,4]{1,0:T(8,128)S(1)}, u32[]{:S(2)}, u32[]{:S(2)}) collective-permute-start(f32[16,4]{1,0:T(8,128)S(1)} %constant_dynamic-slice_fusion.6), channel_id=1, source_target_pairs={{0,4},{4,0},{8,12},{12,8},{16,20},{20,16},{24,28},{28,24},{1,5},{5... | collective-permute-start | bytes 776 | tf_op jit(solution)/shard_map/ppermute | solution.py:15
  102.4 3.8 %collective-permute-start.5 = (f32[16,256]{1,0:T(8,128)S(1)}, f32[16,256]{1,0:T(8,128)S(1)}, u32[]{:S(2)}, u32[]{:S(2)}) collective-permute-start(f32[16,256]{1,0:T(8,128)S(1)} %constant_dynamic-slice_fusion.8), channel_id=1, source_target_pairs={{0,4},{4,0},{8,12},{12,8},{16,20},{20,16},{24,28},{28,24},{1,5},{5... | collective-permute-start | bytes 49160 | tf_op jit(solution)/shard_map/ppermute | solution.py:15
  107.0 72.8 %all-gather.2.cloned.1.call-start = ((), (), s32[]{:S(2)}) async-start(), calls=%async_computation.3 | async-start | bytes 1310720 | tf_op jit(solution)/shard_map/all_gather | solution.py:19
  138.3 3.9 %collective-permute-start.8 = (bf16[16,1024]{1,0:T(8,128)(2,1)S(1)}, bf16[16,1024]{1,0:T(8,128)(2,1)S(1)}, u32[]{:S(2)}, u32[]{:S(2)}) collective-permute-start(bf16[16,1024]{1,0:T(8,128)(2,1)S(1)} %convolution_convert_fusion), channel_id=1, source_target_pairs={{0,4},{4,0},{8,12},{12,8},{16,20},{20,16},{24,28},{28,24},{1,5},{5... | collective-permute-start | bytes 98312 | tf_op jit(solution)/shard_map/ppermute | solution.py:15
  142.2 14.3 %collective-permute-start.9 = (bf16[32,1024]{1,0:T(8,128)(2,1)S(1)}, bf16[32,1024]{1,0:T(8,128)(2,1)S(1)}, u32[]{:S(2)}, u32[]{:S(2)}) collective-permute-start(bf16[32,1024]{1,0:T(8,128)(2,1)S(1)} %maximum_select_fusion.2), channel_id=1, source_target_pairs={{0,8},{4,12},{8,0},{12,4},{16,24},{20,28},{24,16},{28,20},{1,9},{5... | collective-permute-start | bytes 196616 | tf_op jit(solution)/shard_map/ppermute | solution.py:15
  156.8 4.7 %copy-start.1 = (bf16[16,64,16,64]{3,2,1,0:T(8,128)(2,1)S(1)}, bf16[16,64,16,64]{3,2,1,0:T(8,128)(2,1)}, u32[]{:S(2)}) copy-start(bf16[16,64,16,64]{3,2,1,0:T(8,128)(2,1)} %reshape.166) | copy-start | bytes 6291460
  187.0 3.7 %collective-permute-start.10 = (f32[32,16]{0,1:T(8,128)S(1)}, f32[32,16]{0,1:T(8,128)S(1)}, u32[]{:S(2)}, u32[]{:S(2)}) collective-permute-start(f32[32,16]{0,1:T(8,128)S(1)} %constant_dynamic-slice_fusion.5), channel_id=1, source_target_pairs={{0,8},{4,12},{8,0},{12,4},{16,24},{20,28},{24,16},{28,20},{1,9},{5... | collective-permute-start | bytes 6152 | tf_op jit(solution)/shard_map/ppermute | solution.py:15
  188.6 3.7 %collective-permute-start.14 = (f32[32,16]{0,1:T(8,128)S(1)}, f32[32,16]{0,1:T(8,128)S(1)}, u32[]{:S(2)}, u32[]{:S(2)}) collective-permute-start(f32[32,16]{0,1:T(8,128)S(1)} %constant_dynamic-slice_fusion.1), channel_id=1, source_target_pairs={{0,8},{4,12},{8,0},{12,4},{16,24},{20,28},{24,16},{28,20},{1,9},{5... | collective-permute-start | bytes 6152 | tf_op jit(solution)/shard_map/ppermute | solution.py:15
  189.1 6.2 %collective-permute-start.11 = (f32[32,1024]{1,0:T(8,128)S(1)}, f32[32,1024]{1,0:T(8,128)S(1)}, u32[]{:S(2)}, u32[]{:S(2)}) collective-permute-start(f32[32,1024]{1,0:T(8,128)S(1)} %constant_dynamic-slice_fusion.4), channel_id=1, source_target_pairs={{0,8},{4,12},{8,0},{12,4},{16,24},{20,28},{24,16},{28,20},{1,9},{5... | collective-permute-start | bytes 393224 | tf_op jit(solution)/shard_map/ppermute | solution.py:15
  193.1 3.8 %collective-permute-start.12 = (f32[16,16]{0,1:T(8,128)S(1)}, f32[16,16]{0,1:T(8,128)S(1)}, u32[]{:S(2)}, u32[]{:S(2)}) collective-permute-start(f32[16,16]{0,1:T(8,128)S(1)} %constant_dynamic-slice_fusion.3), channel_id=1, source_target_pairs={{0,4},{4,0},{8,12},{12,8},{16,20},{20,16},{24,28},{28,24},{1,5},{5... | collective-permute-start | bytes 3080 | tf_op jit(solution)/shard_map/ppermute | solution.py:15
  194.7 3.7 %collective-permute-start.15 = (f32[16,16]{0,1:T(8,128)S(1)}, f32[16,16]{0,1:T(8,128)S(1)}, u32[]{:S(2)}, u32[]{:S(2)}) collective-permute-start(f32[16,16]{0,1:T(8,128)S(1)} %constant_dynamic-slice_fusion), channel_id=1, source_target_pairs={{0,4},{4,0},{8,12},{12,8},{16,20},{20,16},{24,28},{28,24},{1,5},{5... | collective-permute-start | bytes 3080 | tf_op jit(solution)/shard_map/ppermute | solution.py:15
  195.4 4.3 %collective-permute-start.13 = (f32[16,1024]{1,0:T(8,128)S(1)}, f32[16,1024]{1,0:T(8,128)S(1)}, u32[]{:S(2)}, u32[]{:S(2)}) collective-permute-start(f32[16,1024]{1,0:T(8,128)S(1)} %constant_dynamic-slice_fusion.2), channel_id=1, source_target_pairs={{0,4},{4,0},{8,12},{12,8},{16,20},{20,16},{24,28},{28,24},{1,5},{5... | collective-permute-start | bytes 196616 | tf_op jit(solution)/shard_map/ppermute | solution.py:15
Sparse Core Ops, SparseCore 0:
  13.0 65.3 reduce-scatter.1
  107.1 29.7 all-reduce.1
  163.8 15.9 all-gather.1
where the time goes:
time: 210 us; the launch traced here: 209 us
  waiting for transfers between devices  111 us (53%)
  local copies, waits for them, and re-layouts  26.4 us (13%)
  starting transfers between devices  19.8 us (9%)
  matrix products  19.4 us (9%)
  between operations  14.2 us (7%)
  blocking collectives  10.6 us (5%)
  other arithmetic  7.84 us (4%)
    reduce_scatter x1, waiting for transfers between devices, shards(): lax.psum_scatter(jnp.dot(onehot_table, embedding, preferred_element_type=...  65.4 us
    psum x1, waiting for transfers between devices, shards(): lax.psum(jnp.dot(self_context, output_weight, preferred_element_type=jnp....  29.6 us
    ppermute x16, starting transfers between devices, from_partner(): return lax.ppermute(value, axis, pairs)  19.5 us
    ppermute x16, waiting for transfers between devices, from_partner(): return lax.ppermute(value, axis, pairs)  11.2 us
    all_gather x2, blocking collectives, joined(): everything = jax.tree.map(lambda part: lax.all_gather(part, axis), x)  10.6 us
    reshape x1, local copies, waits for them, and re-layouts, shards(): image_values.reshape(row_count, patch_count, HEADS, head_size)  6.4 us
    reshape x1, local copies, waits for them, and re-layouts, shards(): patch_keys = image_keys.reshape(row_count, patch_count, HEADS, head_size)  6.37 us
    dot_general x1, matrix products, shards(): jnp.dot(onehot_table, embedding, preferred_element_type=jnp.float32)  5.58 us
  transfers between devices with their start and end apart: 19, of which 13 were waited for; matrix products, arithmetic and copies ran while one was open for 11% of the time, Pallas kernels for 0%

commit v1 on v0

--- a/solution.py
+++ b/solution.py
@@ -173,8 +173,11 @@
     ] * value_heads.astype(jnp.float32)
     self_context = weighted / sums[..., None]
     self_context = self_context.reshape(row_count, width_here).astype(jnp.bfloat16)
-    middle = tokens + lax.psum(
-        jnp.dot(self_context, output_weight, preferred_element_type=jnp.float32), "patch"
+    middle = tokens + jnp.sum(
+        lax.all_gather(
+            jnp.dot(self_context, output_weight, preferred_element_type=jnp.float32), "patch"
+        ),
+        axis=0,
     )
     probes = jnp.dot(
         normalize(middle, cross_gain), cross_query, preferred_element_type=jnp.float32

time: 210 us -> 184 us (0.88)
  waiting for transfers between devices: 111 us -> 81.8 us
  blocking collectives: 10.6 us -> 16.6 us
  starting transfers between devices: 19.8 us -> 17.7 us
    psum x1 -> x0, waiting for transfers between devices: 29.6 us -> none  [shards(): lax.psum(jnp.dot(self_context, output_weight, preferred_element_type=jnp....]
    all_gather x0 -> x1, blocking collectives: none -> 5.95 us  [shards(): lax.all_gather(jnp.dot(self_context, output_weight, preferred_element_typ...]
  transfers between devices with their start and end apart: 19 -> 18, of which waited for: 13 -> 12; matrix products, arithmetic and copies ran while one was open for 11% -> 12% of each run, Pallas kernels for 0% -> 0%
where the time goes in v1:
time: 184 us; the launch traced here: 183 us
  waiting for transfers between devices  81.8 us (44%)
  local copies, waits for them, and re-layouts  26.4 us (14%)
  matrix products  18.7 us (10%)
  starting transfers between devices  17.7 us (10%)
  blocking collectives  16.6 us (9%)
  between operations  14.5 us (8%)
  other arithmetic  7.02 us (4%)
    reduce_scatter x1, waiting for transfers between devices, shards(): lax.psum_scatter(jnp.dot(onehot_table, embedding, preferred_element_type=...  65.4 us
    ppermute x16, starting transfers between devices, from_partner(): return lax.ppermute(value, axis, pairs)  17.6 us
    ppermute x16, waiting for transfers between devices, from_partner(): return lax.ppermute(value, axis, pairs)  12.1 us
    all_gather x2, blocking collectives, joined(): everything = jax.tree.map(lambda part: lax.all_gather(part, axis), x)  10.6 us
    reshape x1, local copies, waits for them, and re-layouts, shards(): image_values.reshape(row_count, patch_count, HEADS, head_size)  6.41 us
    reshape x1, local copies, waits for them, and re-layouts, shards(): patch_keys = image_keys.reshape(row_count, patch_count, HEADS, head_size)  6.38 us
    all_gather x1, blocking collectives, shards(): lax.all_gather(jnp.dot(self_context, output_weight, preferred_element_typ...  5.95 us
    dot_general x1, matrix products, shards(): jnp.dot(onehot_table, embedding, preferred_element_type=jnp.float32)  5.58 us
  transfers between devices with their start and end apart: 18, of which 12 were waited for; matrix products, arithmetic and copies ran while one was open for 12% of the time, Pallas kernels for 0%

profile of v1, /device:TPU:0, one launch (start us, length us, event | category | flops | bytes accessed | tf_op | source)
XLA Modules:
  0.0 182.8 jit_solution(8345179263032035695)
XLA Ops:
  7.3 5.6 %fusion.7 = f32[128,1024]{1,0:T(8,128)} fusion(bf16[4000,1024]{1,0:T(8,128)(2,1)} %param.19, s32[4000]{0:T(1024)S(1)} %iota_add_fusion, s32[128]{0:T(128)} %param.17), kind=kOutput, calls=%fused_computation.12 | convolution fusion | flops 1049088000 | bytes 8732800 | tf_op jit(solution)/shard_map/dot_general | solution.py:117
  13.0 65.4 %reduce-scatter.2.cloned.1.call-done = f32[16,1024]{1,0:T(8,128)} async-done(((f32[128,1024]{1,0:T(8,128)}), f32[16,1024]{1,0:T(8,128)}) %reduce-scatter.2.cloned.1.call-update) | async-done | bytes 65552 | tf_op jit(solution)/shard_map/reduce_scatter | solution.py:116
  78.4 1.0 multiply_reduce_fusion.2
  79.4 0.9 multiply_convert_fusion.1
  80.7 1.4 collective-permute-start
  82.1 1.6 copy.108
  83.9 2.3 %copy.114 = bf16[16,128,256]{1,2,0:T(8,128)(2,1)} copy(bf16[16,128,256]{2,1,0:T(8,128)(2,1)} %param.26) | data formatting | bytes 2097152 | tf_op args[9]
  86.2 1.6 collective-permute-start.1
  87.9 1.2 convolution_convert_fusion.1
  89.3 0.9 collective-permute-done.1
  92.0 1.9 %convolution_bitcast_fusion = f32[4,16,4,64]{3,0,2,1:T(4,128)S(1)} fusion(bf16[16,128,4,64]{1,3,2,0:T(8,128)(2,1)} %bitcast.83, f32[4,16,4,128]{3,0,2,1:T(4,128)S(1)} %get-tuple-element.228, f32[4,16]{0,1:T(8,128)S(1)} %copy.113, f32[4,16,4]{0,2,1:T(4,128)S(1)} %copy.112), kind=kOutput, calls=%fused_computation.17 | convolution fusion | flops 4292608 | bytes 1246464 | tf_op jit(solution)/shard_map/bihl,ilhe->bihe/dot_general | solution.py:158
  94.5 1.6 collective-permute-start.2
  96.1 0.5 collective-permute-start.6
  96.6 1.5 collective-permute-start.3
  98.3 1.6 collective-permute-done.6
  100.3 0.6 collective-permute-start.4
  100.9 1.5 collective-permute-start.7
  102.4 0.6 collective-permute-start.5
  103.0 1.0 collective-permute-done.4
  104.0 0.5 collective-permute-done.7
  105.2 1.0 collective-permute-done.5
  106.4 5.9 %all-gather = f32[64,1024]{1,0:T(8,128)S(1)} all-gather(f32[16,1024]{1,0:T(8,128)S(1)} %fusion.41), channel_id=2, replica_groups=mesh['dp'=8,'patch'=4] {'patch'}, dimensions={0}, use_global_device_ids=true | all-gather | bytes 327680 | tf_op jit(solution)/shard_map/all_gather | solution.py:177
  112.9 0.5 collective-permute-start.8
  113.5 3.4 %collective-permute-done.8 = bf16[16,1024]{1,0:T(8,128)(2,1)S(1)} collective-permute-done((bf16[16,1024]{1,0:T(8,128)(2,1)S(1)}, bf16[16,1024]{1,0:T(8,128)(2,1)S(1)}, u32[]{:S(2)}, u32[]{:S(2)}) %collective-permute-start.8) | collective-permute-done | bytes 32800 | tf_op jit(solution)/shard_map/ppermute | solution.py:15
  116.9 0.6 collective-permute-start.9
  117.5 6.4 %reshape.165 = bf16[16,64,16,64]{3,2,1,0:T(8,128)(2,1)} reshape(bf16[1,16,64,1024]{3,2,1,0:T(8,128)(2,1)} %param.30) | data formatting | bytes 4194304 | tf_op jit(solution)/shard_map/reshape | solution.py:187
  123.8 6.4 %reshape.166 = bf16[16,64,16,64]{3,2,1,0:T(8,128)(2,1)} reshape(bf16[1,16,64,1024]{3,2,1,0:T(8,128)(2,1)} %param.31) | data formatting | bytes 4194304 | tf_op jit(solution)/shard_map/reshape | solution.py:188
  130.5 4.7 %fusion.51 = (f32[4,16,16]{0,2,1:T(8,128)S(1)}, f32[4,16,16,64]{3,0,2,1:T(4,128)S(1)}) fusion(bf16[16,64,16,64]{3,2,1,0:T(8,128)(2,1)} %reshape.165, bf16[4,16,16,64]{3,2,1,0:T(8,128)(2,1)S(1)} %select_n.148), kind=kOutput, calls=%fused_computation.109 | convolution fusion | flops 8518656 | bytes 2494464 | tf_op jit(solution)/shard_map/bihe,iphe->bihp/dot_general | solution.py:190
  135.2 1.3 fusion.9
  136.5 0.9 all_gather_reshape.11
  137.6 0.7 fusion.23
  138.6 5.2 %all_gather.18 = f32[4,64,16]{1,2,0:T(8,128)S(1)} all-gather(f32[1,64,16]{1,2,0:T(8,128)S(1)} %all_gather_reshape.10), channel_id=1, replica_groups=mesh['dp'=8,'patch'=4] {'patch'}, dimensions={0}, use_global_device_ids=true | all-gather | bytes 20480 | tf_op jit(solution)/shard_map/all_gather | solution.py:19
  143.8 5.4 %all_gather.17 = f32[4,64,16]{1,2,0:T(8,128)S(1)} all-gather(f32[1,64,16]{1,2,0:T(8,128)S(1)} %all_gather_reshape.9), channel_id=1, replica_groups=mesh['dp'=8,'patch'=4] {'patch'}, dimensions={0}, use_global_device_ids=true | all-gather | bytes 20480 | tf_op jit(solution)/shard_map/all_gather | solution.py:19
  149.2 4.3 %all-gather.3.cloned.1.call-done = f32[4,64,1024]{2,1,0:T(8,128)} async-done(((f32[1,64,1024]{2,1,0:T(8,128)}), f32[4,64,1024]{2,1,0:T(8,128)}) %all-gather.3.cloned.1.call-update) | async-done | bytes 1048592 | tf_op jit(solution)/shard_map/all_gather | solution.py:19
  153.5 1.0 slice_bitcast_fusion
  154.5 6.1 %while.19 = (s32[]{:T(128)}, f32[64,16]{0,1:T(8,128)S(1)}, f32[64,16]{0,1:T(8,128)S(1)}, f32[64,1024]{1,0:T(8,128)S(1)}, f32[4,64,16]{1,2,0:T(8,128)S(1)}, /*ind...) while((s32[]{:T(128)}, f32[64,16]{0,1:T(8,128)S(1)}, ...), condition=%wide.region_11.12_spmd, body=%wide.region_10.11_spmd.sunk | while | flops 202757 | bytes 2941079 | solution.py:25
  155.4 1.1 fusion.67
  157.5 1.1 fusion.67
  159.5 1.1 fusion.67
  160.7 1.5 collective-permute-start.10
  162.2 0.5 collective-permute-start.14
  162.8 1.6 collective-permute-start.11
  164.4 1.6 collective-permute-done.14
  166.8 1.5 collective-permute-start.12
  168.4 0.6 collective-permute-start.15
  169.0 1.5 collective-permute-start.13
  170.6 1.5 collective-permute-done.15
  173.4 2.6 %fusion.19 = bf16[16,1024]{1,0:T(8,128)(2,1)} fusion(f32[16,1024]{1,0:T(8,128)S(1)} %get-tuple-element.210, bf16[1024,1024]{1,0:T(8,128)(2,1)} %param.29, f32[16,1024]{1,0:T(8,128)S(1)} %div.62, f32[16,1024]{1,0:T(8,128)S(1)} %collective-permute-done.13, f32[16,1024]{1,0:T(8,128)S(1)} %mul.400, f32[16,1024]{1,0:T(8,128)S(1)} %mul.397, ...), kind=kOutput, calls=%fused_computation.21 | convolution fusion | flops 33669120 | bytes 2523140 | tf_op jit(solution)/shard_map/dot_general | solution.py:214
  (145 shorter events, 11.3 us)
Async XLA Ops:
  7.2 105.3 %copy-start = (bf16[1024,1024]{1,0:T(8,128)(2,1)S(1)}, bf16[1024,1024]{1,0:T(8,128)(2,1)}, u32[]{:S(2)}) copy-start(bf16[1024,1024]{1,0:T(8,128)(2,1)} %param.28) | copy-start | bytes 6291460
  7.2 71.2 %reduce-scatter.2.cloned.1.call-start = ((), (), s32[]{:S(2)}) async-start(), calls=%async_computation.1 | async-start | bytes 589824 | tf_op jit(solution)/shard_map/reduce_scatter | solution.py:116
  7.2 5.7 %copy-start.8 = (bf16[1024]{0:T(1024)(128)(2,1)S(1)}, bf16[1024]{0:T(1024)(128)(2,1)}, u32[]{:S(2)}) copy-start(bf16[1024]{0:T(1024)(128)(2,1)} %param.20) | copy-start | bytes 6148
  7.3 73.0 %copy-start.5 = (bf16[1024,256]{1,0:T(8,128)(2,1)S(1)}, bf16[1024,256]{1,0:T(8,128)(2,1)}, u32[]{:S(2)}) copy-start(bf16[1024,256]{1,0:T(8,128)(2,1)} %param.21) | copy-start | bytes 1572868
  7.3 73.2 %copy-start.3 = (bf16[1024,256]{1,0:T(8,128)(2,1)S(1)}, bf16[1024,256]{1,0:T(8,128)(2,1)}, u32[]{:S(2)}) copy-start(bf16[1024,256]{1,0:T(8,128)(2,1)} %param.22) | copy-start | bytes 1572868
  7.3 74.8 %copy-start.10 = (s32[128]{0:T(128)S(1)}, s32[128]{0:T(128)}, u32[]{:S(2)}) copy-start(s32[128]{0:T(128)} %param.18) | copy-start | bytes 1540
  12.9 73.3 %copy-start.9 = (bf16[1024]{0:T(1024)(128)(2,1)S(1)}, bf16[1024]{0:T(1024)(128)(2,1)}, u32[]{:S(2)}) copy-start(bf16[1024]{0:T(1024)(128)(2,1)} %param.27) | copy-start | bytes 6148
  12.9 140.6 %all-gather.3.cloned.1.call-start = ((), (), s32[]{:S(2)}) async-start(), calls=%async_computation.2 | async-start | bytes 1310720 | tf_op jit(solution)/shard_map/all_gather | solution.py:19
  80.7 8.6 %copy-start.6 = (bf16[16,256]{1,0:T(8,128)(2,1)}, bf16[16,256]{1,0:T(8,128)(2,1)S(1)}, u32[]{:S(2)}) copy-start(bf16[16,256]{1,0:T(8,128)(2,1)S(1)} %get-tuple-element.230) | copy-start | bytes 24580
  80.7 5.5 %collective-permute-start = (bf16[2,16,256]{2,1,0:T(8,128)(2,1)S(1)}, bf16[2,16,256]{2,1,0:T(8,128)(2,1)S(1)}, u32[]{:S(2)}, u32[]{:S(2)}) collective-permute-start(bf16[2,16,256]{2,1,0:T(8,128)(2,1)S(1)} %pad_maximum_fusion), channel_id=1, source_target_pairs={{0,4},{4,0},{8,12},{12,8},{16,20},{20,16},{24,28},{28,24},{1,5},{5... | collective-permute-start | bytes 49160 | tf_op jit(solution)/shard_map/ppermute | solution.py:15
  86.2 26.2 %copy-start.2 = (f32[16,1024]{1,0:T(8,128)S(1)}, f32[16,1024]{1,0:T(8,128)}, u32[]{:S(2)}) copy-start(f32[16,1024]{1,0:T(8,128)} %reduce-scatter.2.cloned.1.call-done) | copy-start | bytes 196612
  86.2 4.0 %collective-permute-start.1 = (bf16[2,32,256]{2,1,0:T(8,128)(2,1)S(1)}, bf16[2,32,256]{2,1,0:T(8,128)(2,1)S(1)}, u32[]{:S(2)}, u32[]{:S(2)}) collective-permute-start(bf16[2,32,256]{2,1,0:T(8,128)(2,1)S(1)} %maximum_select_fusion.3), channel_id=1, source_target_pairs={{0,8},{4,12},{8,0},{12,4},{16,24},{20,28},{24,16},{28,20},{1,9},{5... | collective-permute-start | bytes 98312 | tf_op jit(solution)/shard_map/ppermute | solution.py:15
  89.1 23.9 %copy-start.7 = (bf16[16,256]{1,0:T(8,128)(2,1)}, bf16[16,256]{1,0:T(8,128)(2,1)S(1)}, u32[]{:S(2)}) copy-start(bf16[16,256]{1,0:T(8,128)(2,1)S(1)} %convolution_convert_fusion.1) | copy-start | bytes 24580
  90.8 15.4 %copy-start.4 = (bf16[256,1024]{1,0:T(8,128)(2,1)S(1)}, bf16[256,1024]{1,0:T(8,128)(2,1)}, u32[]{:S(2)}) copy-start(bf16[256,1024]{1,0:T(8,128)(2,1)} %param.24) | copy-start | bytes 1572868
  94.5 3.8 %collective-permute-start.2 = (f32[32,4]{1,0:T(8,128)S(1)}, f32[32,4]{1,0:T(8,128)S(1)}, u32[]{:S(2)}, u32[]{:S(2)}) collective-permute-start(f32[32,4]{1,0:T(8,128)S(1)} %constant_dynamic-slice_fusion.11), channel_id=1, source_target_pairs={{0,8},{4,12},{8,0},{12,4},{16,24},{20,28},{24,16},{28,20},{1,9},{5... | collective-permute-start | bytes 1544 | tf_op jit(solution)/shard_map/ppermute | solution.py:15
  96.1 3.7 %collective-permute-start.6 = (f32[32,4]{1,0:T(8,128)S(1)}, f32[32,4]{1,0:T(8,128)S(1)}, u32[]{:S(2)}, u32[]{:S(2)}) collective-permute-start(f32[32,4]{1,0:T(8,128)S(1)} %constant_dynamic-slice_fusion.7), channel_id=1, source_target_pairs={{0,8},{4,12},{8,0},{12,4},{16,24},{20,28},{24,16},{28,20},{1,9},{5... | collective-permute-start | bytes 1544 | tf_op jit(solution)/shard_map/ppermute | solution.py:15
  96.6 5.8 %collective-permute-start.3 = (f32[32,256]{1,0:T(8,128)S(1)}, f32[32,256]{1,0:T(8,128)S(1)}, u32[]{:S(2)}, u32[]{:S(2)}) collective-permute-start(f32[32,256]{1,0:T(8,128)S(1)} %constant_dynamic-slice_fusion.10), channel_id=1, source_target_pairs={{0,8},{4,12},{8,0},{12,4},{16,24},{20,28},{24,16},{28,20},{1,9},{5... | collective-permute-start | bytes 98312 | tf_op jit(solution)/shard_map/ppermute | solution.py:15
  100.3 3.7 %collective-permute-start.4 = (f32[16,4]{1,0:T(8,128)S(1)}, f32[16,4]{1,0:T(8,128)S(1)}, u32[]{:S(2)}, u32[]{:S(2)}) collective-permute-start(f32[16,4]{1,0:T(8,128)S(1)} %constant_dynamic-slice_fusion.9), channel_id=1, source_target_pairs={{0,4},{4,0},{8,12},{12,8},{16,20},{20,16},{24,28},{28,24},{1,5},{5... | collective-permute-start | bytes 776 | tf_op jit(solution)/shard_map/ppermute | solution.py:15
  100.9 3.7 %collective-permute-start.7 = (f32[16,4]{1,0:T(8,128)S(1)}, f32[16,4]{1,0:T(8,128)S(1)}, u32[]{:S(2)}, u32[]{:S(2)}) collective-permute-start(f32[16,4]{1,0:T(8,128)S(1)} %constant_dynamic-slice_fusion.6), channel_id=1, source_target_pairs={{0,4},{4,0},{8,12},{12,8},{16,20},{20,16},{24,28},{28,24},{1,5},{5... | collective-permute-start | bytes 776 | tf_op jit(solution)/shard_map/ppermute | solution.py:15
  102.4 3.8 %collective-permute-start.5 = (f32[16,256]{1,0:T(8,128)S(1)}, f32[16,256]{1,0:T(8,128)S(1)}, u32[]{:S(2)}, u32[]{:S(2)}) collective-permute-start(f32[16,256]{1,0:T(8,128)S(1)} %constant_dynamic-slice_fusion.8), channel_id=1, source_target_pairs={{0,4},{4,0},{8,12},{12,8},{16,20},{20,16},{24,28},{28,24},{1,5},{5... | collective-permute-start | bytes 49160 | tf_op jit(solution)/shard_map/ppermute | solution.py:15
  112.9 3.9 %collective-permute-start.8 = (bf16[16,1024]{1,0:T(8,128)(2,1)S(1)}, bf16[16,1024]{1,0:T(8,128)(2,1)S(1)}, u32[]{:S(2)}, u32[]{:S(2)}) collective-permute-start(bf16[16,1024]{1,0:T(8,128)(2,1)S(1)} %convolution_convert_fusion), channel_id=1, source_target_pairs={{0,4},{4,0},{8,12},{12,8},{16,20},{20,16},{24,28},{28,24},{1,5},{5... | collective-permute-start | bytes 98312 | tf_op jit(solution)/shard_map/ppermute | solution.py:15
  116.9 13.4 %collective-permute-start.9 = (bf16[32,1024]{1,0:T(8,128)(2,1)S(1)}, bf16[32,1024]{1,0:T(8,128)(2,1)S(1)}, u32[]{:S(2)}, u32[]{:S(2)}) collective-permute-start(bf16[32,1024]{1,0:T(8,128)(2,1)S(1)} %maximum_select_fusion.2), channel_id=1, source_target_pairs={{0,8},{4,12},{8,0},{12,4},{16,24},{20,28},{24,16},{28,20},{1,9},{5... | collective-permute-start | bytes 196616 | tf_op jit(solution)/shard_map/ppermute | solution.py:15
  130.5 4.7 %copy-start.1 = (bf16[16,64,16,64]{3,2,1,0:T(8,128)(2,1)S(1)}, bf16[16,64,16,64]{3,2,1,0:T(8,128)(2,1)}, u32[]{:S(2)}) copy-start(bf16[16,64,16,64]{3,2,1,0:T(8,128)(2,1)} %reshape.166) | copy-start | bytes 6291460
  160.7 3.7 %collective-permute-start.10 = (f32[32,16]{0,1:T(8,128)S(1)}, f32[32,16]{0,1:T(8,128)S(1)}, u32[]{:S(2)}, u32[]{:S(2)}) collective-permute-start(f32[32,16]{0,1:T(8,128)S(1)} %constant_dynamic-slice_fusion.5), channel_id=1, source_target_pairs={{0,8},{4,12},{8,0},{12,4},{16,24},{20,28},{24,16},{28,20},{1,9},{5... | collective-permute-start | bytes 6152 | tf_op jit(solution)/shard_map/ppermute | solution.py:15
  162.2 3.7 %collective-permute-start.14 = (f32[32,16]{0,1:T(8,128)S(1)}, f32[32,16]{0,1:T(8,128)S(1)}, u32[]{:S(2)}, u32[]{:S(2)}) collective-permute-start(f32[32,16]{0,1:T(8,128)S(1)} %constant_dynamic-slice_fusion.1), channel_id=1, source_target_pairs={{0,8},{4,12},{8,0},{12,4},{16,24},{20,28},{24,16},{28,20},{1,9},{5... | collective-permute-start | bytes 6152 | tf_op jit(solution)/shard_map/ppermute | solution.py:15
  162.8 6.2 %collective-permute-start.11 = (f32[32,1024]{1,0:T(8,128)S(1)}, f32[32,1024]{1,0:T(8,128)S(1)}, u32[]{:S(2)}, u32[]{:S(2)}) collective-permute-start(f32[32,1024]{1,0:T(8,128)S(1)} %constant_dynamic-slice_fusion.4), channel_id=1, source_target_pairs={{0,8},{4,12},{8,0},{12,4},{16,24},{20,28},{24,16},{28,20},{1,9},{5... | collective-permute-start | bytes 393224 | tf_op jit(solution)/shard_map/ppermute | solution.py:15
  166.8 3.8 %collective-permute-start.12 = (f32[16,16]{0,1:T(8,128)S(1)}, f32[16,16]{0,1:T(8,128)S(1)}, u32[]{:S(2)}, u32[]{:S(2)}) collective-permute-start(f32[16,16]{0,1:T(8,128)S(1)} %constant_dynamic-slice_fusion.3), channel_id=1, source_target_pairs={{0,4},{4,0},{8,12},{12,8},{16,20},{20,16},{24,28},{28,24},{1,5},{5... | collective-permute-start | bytes 3080 | tf_op jit(solution)/shard_map/ppermute | solution.py:15
  168.4 3.7 %collective-permute-start.15 = (f32[16,16]{0,1:T(8,128)S(1)}, f32[16,16]{0,1:T(8,128)S(1)}, u32[]{:S(2)}, u32[]{:S(2)}) collective-permute-start(f32[16,16]{0,1:T(8,128)S(1)} %constant_dynamic-slice_fusion), channel_id=1, source_target_pairs={{0,4},{4,0},{8,12},{12,8},{16,20},{20,16},{24,28},{28,24},{1,5},{5... | collective-permute-start | bytes 3080 | tf_op jit(solution)/shard_map/ppermute | solution.py:15
  169.0 4.3 %collective-permute-start.13 = (f32[16,1024]{1,0:T(8,128)S(1)}, f32[16,1024]{1,0:T(8,128)S(1)}, u32[]{:S(2)}, u32[]{:S(2)}) collective-permute-start(f32[16,1024]{1,0:T(8,128)S(1)} %constant_dynamic-slice_fusion.2), channel_id=1, source_target_pairs={{0,4},{4,0},{8,12},{12,8},{16,20},{20,16},{24,28},{28,24},{1,5},{5... | collective-permute-start | bytes 196616 | tf_op jit(solution)/shard_map/ppermute | solution.py:15
Sparse Core Ops, SparseCore 0:
  13.0 65.3 reduce-scatter.1
  137.5 15.9 all-gather.2
